TPU v7x, 32 devices: a whole 2x2x4 slice. The times are simulated.
32 devices in a mesh: seq: 8 (over z, core), tp: 4 (over y, x).
Axes of the slice: x: 2, y: 2, z: 4, core: 2. Of those that a mesh axis runs over, the one named last changes fastest.
Arguments:
- hidden: bfloat16 [4096, 2048], P(('seq', 'tp')), may hold values from -5 to 5
- w_qkv: bfloat16 [2048, 3, 2048], P(None, None, 'tp'), may hold values from -0.125 to 0.125
- w_gate: bfloat16 [2048, 2048], P(None, 'tp'), may hold values from -0.125 to 0.125
- w_decay_beta: bfloat16 [2048, 2, 16], P(None, None, 'tp'), may hold values from -0.7 to 0.7
- conv_weight: bfloat16 [4, 3, 2048], P(None, None, 'tp'), may hold values from -2 to 2
- decay_rate: float32 [16], P('tp'), may hold values from 2e-05 to 0.05
- dt_bias: float32 [16], P('tp'), may hold values from -1 to 1
- norm_gain: float32 [128], replicated, may hold values from 0.1 to 1.9
Outputs:
- core: bfloat16 [4096, 2048], P('seq', 'tp')
All inputs are finite; a program needn't handle non-finite values.
Results may differ from a plain program's by a relative error of at most 0.01.
Values may be sent and summed in bfloat16 or wider, within the bound.
A program may use at most 64 MiB of HBM per device.

v0:
```python
import functools
import math

import jax
import jax.numpy as jnp
from jax import lax
from jax.experimental import pallas as pl
from jax.experimental.pallas import tpu as pltpu
from jax.sharding import PartitionSpec as P

MESH = pl.DeviceIdType.MESH
CHUNK = 128
RIM = 16
NT = (((1,), (1,)), ((), ()))
TN = (((0,), (0,)), ((), ()))


def low(value):
    return value.astype(jnp.bfloat16)


def dot(left, right, dims=(((1,), (0,)), ((), ()))):
    return lax.dot_general(low(left), low(right), dims, preferred_element_type=jnp.float32)


def peer_of(me, step, count):
    if count & (count - 1):
        return lax.rem(me + step, count)
    bit = 1
    while bit < count:
        if step & bit:
            me = me + bit - 2 * bit * lax.rem(me // bit, 2)
        bit *= 2
    return me


def silu(value):
    return value / (1.0 + jnp.exp(-value))


def unit_rows(matrix):
    return matrix * lax.rsqrt(jnp.sum(matrix * matrix, axis=-1, keepdims=True) + 1e-06)


def kernel(
    n_seq, n_tp, rate_hbm, bias_hbm, hidden, w_qkv, w_gate, wdb_hbm, conv_hbm, gain_hbm, out_ref,
    rate_ref, bias_ref, wdb_ref, conv_ref, gain_ref, small_sem,
    tokens, rim, weights, proj, state, outs, deltas, st_in, st_out,
    tok_send, tok_recv, w_sem, rim_send, rim_recv, st_send, st_recv,
    middle, mid_send, mid_recv, solves, q_runs, k_tails, attends, fades,
):
    seq, me = lax.axis_index("seq"), lax.axis_index("tp")
    rows = hidden.shape[0]
    total = tokens.shape[0]
    heads = rate_ref.shape[1]
    head_dim = gain_ref.shape[1]
    taps = conv_ref.shape[1]
    last_tp, last_seq = n_tp - 1, n_seq - 1
    square = n_tp == 4 and rows == CHUNK
    part = rows // 2

    own = pltpu.make_async_copy(hidden, tokens.at[pl.ds(me * rows, rows)], tok_recv.at[0, 0])
    own.start()
    loads = [pltpu.make_async_copy(w_qkv.at[b], weights.at[b], w_sem.at[b]) for b in range(3)]
    loads.append(pltpu.make_async_copy(w_gate, weights.at[3], w_sem.at[3]))
    small = [(rate_hbm, rate_ref), (bias_hbm, bias_ref), (wdb_hbm, wdb_ref), (conv_hbm, conv_ref), (gain_hbm, gain_ref)]
    smalls = [pltpu.make_async_copy(src, dst, small_sem.at[i]) for i, (src, dst) in enumerate(small)]
    for load in loads + smalls:
        load.start()

    barrier = pltpu.get_barrier_semaphore()

    def greet(where):
        pl.semaphore_signal(barrier, inc=1, device_id=where, device_id_type=MESH)

    for step in range(1, n_tp):
        greet({"tp": peer_of(me, step, n_tp)})

    @pl.when(seq > 0)
    def _():
        greet({"seq": seq - 1})

        @pl.when(me < last_tp)
        def _():
            greet({"seq": seq - 1, "tp": last_tp})

    @pl.when(seq < last_seq)
    def _():
        greet({"seq": seq + 1})

    before = (seq + last_seq) // n_seq
    after = (2 * last_seq - seq) // n_seq
    tail_owner = (me + 1) // n_tp
    pl.semaphore_wait(barrier, last_tp + before + after + after * tail_owner * last_tp)

    def token_copy(step):
        return pltpu.make_async_remote_copy(
            src_ref=hidden,
            dst_ref=tokens.at[pl.ds(me * rows, rows)],
            send_sem=tok_send.at[step, 0],
            recv_sem=tok_recv.at[step, 0],
            device_id={"tp": peer_of(me, step, n_tp)},
            device_id_type=MESH,
        )

    def part_copy(step, half):
        return pltpu.make_async_remote_copy(
            src_ref=hidden.at[pl.ds(half * part, part)],
            dst_ref=tokens.at[pl.ds(me * rows + half * part, part)],
            send_sem=tok_send.at[step, half],
            recv_sem=tok_recv.at[step, half],
            device_id={"tp": peer_of(me, step, n_tp)},
            device_id_type=MESH,
        )

    def relay_copy(half):
        there = tokens.at[pl.ds(peer_of(me, 2 - half, n_tp) * rows + half * part, part)]
        return pltpu.make_async_remote_copy(
            src_ref=there,
            dst_ref=there,
            send_sem=tok_send.at[3, half],
            recv_sem=tok_recv.at[3, half],
            device_id={"tp": peer_of(me, 1 + half, n_tp)},
            device_id_type=MESH,
        )

    def middle_copy(target):
        return pltpu.make_async_remote_copy(
            src_ref=hidden.at[pl.ds(rows - RIM, RIM)],
            dst_ref=middle,
            send_sem=mid_send.at[target - 2],
            recv_sem=mid_recv,
            device_id={"tp": target},
            device_id_type=MESH,
        )

    def rim_copy(target):
        return pltpu.make_async_remote_copy(
            src_ref=hidden.at[pl.ds(rows - RIM, RIM)],
            dst_ref=rim,
            send_sem=rim_send.at[target],
            recv_sem=rim_recv,
            device_id={"seq": seq + 1, "tp": target},
            device_id_type=MESH,
        )

    @pl.when(jnp.logical_and(seq < last_seq, me == last_tp))
    def _():
        for target in range(n_tp):
            rim_copy(target).start()

    if square:

        @pl.when(me == 1)
        def _():
            for target in (2, 3):
                middle_copy(target).start()

        for step, half in ((1, 1), (2, 0), (1, 0), (2, 1)):
            part_copy(step, half).start()
    else:
        for step in range(1, n_tp):
            token_copy(step).start()

    @pl.when(seq == 0)
    def _():
        rim[...] = jnp.zeros_like(rim)
        st_in[...] = jnp.zeros_like(st_in)

    for load in loads + smalls:
        load.wait()

    def project(block, at):
        def one(b, carry):
            full = jnp.dot(block, weights[b], preferred_element_type=jnp.float32)
            rounded = full.astype(jnp.bfloat16).astype(jnp.float32)
            proj[b, pl.ds(pl.multiple_of(at, 16), block.shape[0]), :] = jnp.where(b < 3, rounded, full)
            return carry

        lax.fori_loop(0, 4, one, 0)

    def project_slot(slot):
        at = pl.multiple_of(slot * rows, 16)
        project(tokens[pl.ds(at, rows), :], RIM + at)

    def project_rim():
        @pl.when(seq > 0)
        def _():
            pltpu.make_async_copy(hidden.at[pl.ds(0, RIM)], rim, rim_recv).wait()

        project(rim[...], 0)

    down = lax.broadcasted_iota(jnp.int32, (CHUNK, CHUNK), 0)
    across = lax.broadcasted_iota(jnp.int32, (CHUNK, CHUNK), 1)
    eye = (down == across).astype(jnp.float32)
    wide = lax.broadcasted_iota(jnp.int32, (head_dim, 2 * head_dim), 0) + head_dim
    start = (wide == lax.broadcasted_iota(jnp.int32, (head_dim, 2 * head_dim), 1)).astype(jnp.float32)
    for h in range(heads):
        state[h] = start

    wdb = low(jnp.concatenate([wdb_ref[0].astype(jnp.float32), wdb_ref[1].astype(jnp.float32)], axis=0))

    def prepare(c):
        r0 = pl.multiple_of(c * CHUNK, CHUNK)
        scalars = lax.dot_general(
            wdb, tokens[pl.ds(r0, CHUNK), :], NT, preferred_element_type=jnp.float32
        )
        per_head = []
        for h in range(heads):
            cols = slice(h * head_dim, (h + 1) * head_dim)
            branch = []
            for b in range(3):
                window = proj[b, pl.ds(r0 + 8, CHUNK + 8), cols]
                conv = jnp.zeros((CHUNK, head_dim), jnp.float32)
                for i in range(taps):
                    offset = 9 - taps + i
                    tap = conv_ref[b, i : i + 1, cols].astype(jnp.float32)
                    conv = conv + window[offset : offset + CHUNK] * tap
                branch.append(silu(conv).astype(jnp.bfloat16).astype(jnp.float32))
            q = unit_rows(branch[0]) * (1.0 / math.sqrt(head_dim))
            k = unit_rows(branch[1])
            v = branch[2]
            u = scalars[h : h + 1, :] + bias_ref[0:1, h : h + 1]
            log_row = -rate_ref[0:1, h : h + 1] * (jnp.maximum(u, 0.0) + jnp.log1p(jnp.exp(-jnp.abs(u))))
            rate_row = 1.0 / (1.0 + jnp.exp(-scalars[heads + h : heads + h + 1, :]))
            cum_col = jnp.sum(jnp.where(across <= down, log_row, 0.0), axis=1, keepdims=True)
            cum_row = jnp.sum(jnp.where(across == down, cum_col, 0.0), axis=0, keepdims=True)
            rate_col = jnp.sum(jnp.where(across == down, rate_row, 0.0), axis=1, keepdims=True)
            end = cum_col[CHUNK - 1 : CHUNK, :]
            gap = jnp.exp(jnp.where(across <= down, cum_col - cum_row, 0.0))
            weight = jnp.where(across <= down, gap, 0.0) * rate_row
            mixing = jnp.where(across < down, weight * dot(k, k, NT), 0.0)
            attend = weight * dot(q, k, NT)
            run = jnp.exp(cum_col)
            tail = rate_col * jnp.exp(end - cum_col)
            q_runs[c, h] = low(q * run)
            k_tails[c, h] = low(k * tail)
            attends[c, h] = low(attend)
            fades[c, h] = jnp.broadcast_to(jnp.exp(end), (1, head_dim))
            per_head.append((mixing, low(jnp.concatenate([v, k * run], axis=1))))
        return per_head

    def local(chunks):
        chains = [(c, h) + item for c in chunks for h, item in enumerate(prepare(c))]
        inverse = [None] * len(chains)
        size = 1
        while size < CHUNK:
            half = (down // size) % 2 == 1
            lower = jnp.logical_and(half, across // size == down // size - 1)
            for i, (_, _, mixing, _) in enumerate(chains):
                corner = jnp.where(lower, mixing, 0.0)
                if size == 1:
                    inverse[i] = eye - corner
                else:
                    inverse[i] = inverse[i] - dot(dot(inverse[i], corner), inverse[i])
            size *= 2
        for i, (c, h, _, right) in enumerate(chains):
            solves[c, h] = dot(inverse[i], right)

    def advance(c, carry):
        r0 = pl.multiple_of(c * CHUNK, CHUNK)
        for h in range(heads):
            solved = solves[c, h]
            held = state[h]
            fresh = solved[:, :head_dim]
            fresh = jnp.concatenate([fresh, jnp.zeros_like(fresh)], axis=1)
            fresh = fresh - dot(solved[:, head_dim:], held)
            read = dot(q_runs[c, h], held) + dot(attends[c, h], fresh)
            fade = jnp.concatenate([fades[c, h]] * 2, axis=1)
            state[h] = fade * held + dot(k_tails[c, h], fresh, TN)
            outs[h, pl.ds(r0, CHUNK), :] = read[:, :head_dim]
            deltas[h, pl.ds(r0, CHUNK), :] = low(read[:, head_dim:])
        return carry

    count = total // CHUNK
    own.wait()
    project_slot(me)
    if square:
        part_copy(1, 1).wait_recv()
        relay_copy(1).start()
        part_copy(2, 0).wait_recv()
        relay_copy(0).start()
        project_rim()

        @pl.when(me >= 2)
        def _():
            pltpu.make_async_copy(hidden.at[pl.ds(0, RIM)], middle, mid_recv).wait()
            project(middle[...], 2 * rows)

        part_copy(1, 0).wait_recv()
        project_slot(peer_of(me, 1, n_tp))
        first = 2 * (me // 2)
        local((first, first + 1))
        part_copy(2, 1).wait_recv()
        project_slot(peer_of(me, 2, n_tp))
        relay_copy(0).wait_recv()
        relay_copy(1).wait_recv()
        project_slot(peer_of(me, 3, n_tp))
        local((2 - first, 3 - first))
    else:
        for step in range(1, n_tp):
            token_copy(step).wait_recv()
            if n_tp & (n_tp - 1):
                project_slot(lax.rem(me - step + n_tp, n_tp))
            else:
                project_slot(peer_of(me, step, n_tp))
        project_rim()
        lax.fori_loop(0, count, lambda c, carry: (local((c,)), carry)[1], 0)
    lax.fori_loop(0, count, advance, 0, unroll=True)

    def state_copy(h):
        return pltpu.make_async_remote_copy(
            src_ref=st_out.at[h],
            dst_ref=st_in.at[h],
            send_sem=st_send.at[h],
            recv_sem=st_recv.at[h],
            device_id={"seq": seq + 1},
            device_id_type=MESH,
        )

    for h in range(heads):

        @pl.when(seq > 0)
        def _():
            pltpu.make_async_copy(st_out.at[h], st_in.at[h], st_recv.at[h]).wait()

        @pl.when(seq < last_seq)
        def _():
            mine = state[h]
            st_out[h] = low(mine[:, :head_dim] + dot(mine[:, head_dim:], st_in[h]))
            state_copy(h).start()

    for h in range(heads):
        cols = slice(h * head_dim, (h + 1) * head_dim)
        read = outs[h] + dot(deltas[h], st_in[h])
        scale = lax.rsqrt(jnp.mean(read * read, axis=-1, keepdims=True) + 1e-06)
        gate = silu(proj[3, pl.ds(RIM, total), cols])
        out_ref[:, cols] = low(read * scale * gain_ref[...] * gate)

    if square:
        for half in range(2):
            part_copy(1, half).wait_send()
            part_copy(2, half).wait_send()
            relay_copy(half).wait_send()

        @pl.when(me == 1)
        def _():
            for target in (2, 3):
                middle_copy(target).wait_send()
    else:
        for step in range(1, n_tp):
            token_copy(step).wait_send()

    @pl.when(jnp.logical_and(seq < last_seq, me == last_tp))
    def _():
        for target in range(n_tp):
            rim_copy(target).wait_send()

    @pl.when(seq < last_seq)
    def _():
        for h in range(heads):
            state_copy(h).wait_send()


def per_device(
    n_seq, n_tp, hidden, w_qkv, w_gate, w_decay_beta, conv_weight, decay_rate, dt_bias, norm_gain
):
    width = hidden.shape[1]
    heads = decay_rate.shape[0]
    head_dim = norm_gain.shape[0]
    columns = heads * head_dim
    rows = hidden.shape[0]
    total = rows * n_tp
    vmem, anywhere = pl.BlockSpec(memory_space=pltpu.VMEM), pl.BlockSpec(memory_space=pl.ANY)
    dma = pltpu.SemaphoreType.DMA
    count = total // CHUNK
    return pl.pallas_call(
        functools.partial(kernel, n_seq, n_tp),
        out_shape=jax.ShapeDtypeStruct((total, columns), jnp.bfloat16),
        in_specs=[anywhere] * 8,
        out_specs=vmem,
        scratch_shapes=[
            pltpu.VMEM((1, heads), jnp.float32),
            pltpu.VMEM((1, heads), jnp.float32),
            pltpu.VMEM((2, heads, width), jnp.bfloat16),
            pltpu.VMEM((3, conv_weight.shape[0], columns), jnp.bfloat16),
            pltpu.VMEM((1, head_dim), jnp.float32),
            dma((5,)),
            pltpu.VMEM((total, width), jnp.bfloat16),
            pltpu.VMEM((RIM, width), jnp.bfloat16),
            pltpu.VMEM((4, width, columns), jnp.bfloat16),
            pltpu.VMEM((4, RIM + total, columns), jnp.float32),
            pltpu.VMEM((heads, head_dim, 2 * head_dim), jnp.float32),
            pltpu.VMEM((heads, total, head_dim), jnp.float32),
            pltpu.VMEM((heads, total, head_dim), jnp.bfloat16),
            pltpu.VMEM((heads, head_dim, head_dim), jnp.bfloat16),
            pltpu.VMEM((heads, head_dim, head_dim), jnp.bfloat16),
            dma((n_tp, 2)),
            dma((n_tp, 2)),
            dma((4,)),
            dma((n_tp,)),
            dma,
            dma((heads,)),
            dma((heads,)),
            pltpu.VMEM((RIM, width), jnp.bfloat16),
            dma((2,)),
            dma,
            pltpu.VMEM((count, heads, CHUNK, 2 * head_dim), jnp.float32),
            pltpu.VMEM((count, heads, CHUNK, head_dim), jnp.bfloat16),
            pltpu.VMEM((count, heads, CHUNK, head_dim), jnp.bfloat16),
            pltpu.VMEM((count, heads, CHUNK, CHUNK), jnp.bfloat16),
            pltpu.VMEM((count, heads, 1, head_dim), jnp.float32),
        ],
        compiler_params=pltpu.CompilerParams(
            collective_id=0, has_side_effects=True, vmem_limit_bytes=60 * 1024 * 1024
        ),
    )(
        decay_rate.reshape(1, heads), dt_bias.reshape(1, heads), hidden,
        w_qkv.transpose(1, 0, 2), w_gate, w_decay_beta.transpose(1, 2, 0),
        conv_weight.transpose(1, 0, 2), norm_gain.reshape(1, head_dim),
    )


def solution(mesh):
    return jax.shard_map(
        functools.partial(per_device, mesh.shape["seq"], mesh.shape["tp"]),
        mesh=mesh,
        in_specs=(
            P(("seq", "tp"), None),
            P(None, None, "tp"),
            P(None, "tp"),
            P(None, None, "tp"),
            P(None, None, "tp"),
            P("tp"),
            P("tp"),
            P(),
        ),
        out_specs=P("seq", "tp"),
        check_vma=False,
    )
```

profile of v0, /device:TPU:25, one launch (start us, length us, event | category | flops | bytes accessed | tf_op | source)
XLA Modules:
  0.0 49.6 jit_solution(17044986851741086416)
XLA Ops:
  0.0 47.7 %shard_map.82 = bf16[512,512]{1,0:T(8,128)(2,1)} custom-call(f32[1,4]{1,0:T(1,128)} %bitcast.9, f32[1,4]{1,0:T(1,128)} %bitcast.10, bf16[128,2048]{1,0:T(8,128)(2,1)} %hidden.1, bf16[3,2048,512]{2,1,0:T(8,128)(2,1)} %bitcast.6, bf16[2048,512]{1,0:T(8,128)(2,1)} %w_gate.1, bf16[2,4,2048]{2,1,0:T(4,128)(2,1)} %bitcast.7, bf16[3,4,512]{2,1,0:T(4,128)(2,1)} %bitcast.8, ...), custom_call_target="tpu_custom_call" | custom-call | tf_op jit(solution)/shard_map/pallas_call | solution.py:377
  47.7 1.9 %copy.10 = bf16[512,512]{1,0:T(8,128)(2,1)} copy(bf16[512,512]{1,0:T(8,128)(2,1)} %shard_map.82) | data formatting | bytes 1048576
where the time goes:
time: 49.7 us; the launch traced here: 49.6 us
  Pallas kernels  47.7 us (96%)
  local copies, waits for them, and re-layouts  1.87 us (4%)
    pallas_call x1, Pallas kernels, per_device(): pl.pallas_call(functools.partial(kernel, n_seq, n_tp), out_shape=jax.Shap...  47.7 us
    unnamed x1, local copies, waits for them, and re-layouts  1.87 us

commit v1 on v0

--- a/solution.py
+++ b/solution.py
@@ -362,7 +362,7 @@
             state_copy(h).wait_send()
 
 
-def per_device(
+def plain_device(
     n_seq, n_tp, hidden, w_qkv, w_gate, w_decay_beta, conv_weight, decay_rate, dt_bias, norm_gain
 ):
     width = hidden.shape[1]
@@ -421,6 +421,510 @@
     )
 
 
+def fast_kernel(
+    n_seq, rate_hbm, bias_hbm, hidden, w_qkv, w_gate, wdb_hbm, conv_hbm, gain_hbm, out_ref,
+    rate_ref, bias_ref, wdb_ref, conv_ref, gain_ref, small_sem,
+    tokens, rim, weights, proj, gates, half_taps, masks,
+    own_sem, tok_send, tok_recv, w_sem, rim_send, rim_recv,
+    lows, rights, keys, tails, decays, runs, fades, solves, maps, prefixes, totals, qeffs, outs, deltas,
+    map_out, map_in, fade_out, fade_in, joined, joined_b, joined_f,
+    map_send, map_recv, fade_send, fade_recv,
+    st_in, st_out, held, st_send, st_recv, fw_send,
+):
+    seq, me = lax.axis_index("seq"), lax.axis_index("tp")
+    last_seq = n_seq - 1
+    odd = lax.rem(seq, 2) == 1
+    even = lax.rem(seq, 2) == 0
+    rows = hidden.shape[0]
+    total = tokens.shape[0]
+    heads = rate_ref.shape[1]
+    dim = gain_ref.shape[1]
+    taps = conv_ref.shape[1]
+    count = total // CHUNK
+    split = 48
+    tail_at = rows - RIM
+
+    own = pltpu.make_async_copy(hidden, tokens.at[pl.ds(me * rows, rows)], own_sem)
+    own.start()
+    order = (1, 2, 0)
+    loads = [pltpu.make_async_copy(w_qkv.at[b], weights.at[i], w_sem.at[i]) for i, b in enumerate(order)]
+    loads.append(pltpu.make_async_copy(w_gate, weights.at[3], w_sem.at[3]))
+    small = [(rate_hbm, rate_ref), (bias_hbm, bias_ref), (wdb_hbm, wdb_ref), (conv_hbm, conv_ref), (gain_hbm, gain_ref)]
+    smalls = [pltpu.make_async_copy(src, dst, small_sem.at[i]) for i, (src, dst) in enumerate(small)]
+    for load in loads + smalls:
+        load.start()
+
+    barrier = pltpu.get_barrier_semaphore()
+
+    def greet(where):
+        pl.semaphore_signal(barrier, inc=1, device_id=where, device_id_type=MESH)
+
+    peers = [peer_of(me, step, 4) for step in range(4)]
+    for step in range(1, 4):
+        greet({"tp": peers[step]})
+
+    @pl.when(seq > 0)
+    def _():
+        greet({"seq": seq - 1})
+
+    @pl.when(seq < last_seq)
+    def _():
+        greet({"seq": seq + 1})
+
+    @pl.when(jnp.logical_and(odd, seq > 1))
+    def _():
+        greet({"seq": seq - 2})
+
+    @pl.when(jnp.logical_and(odd, seq < last_seq))
+    def _():
+        greet({"seq": seq + 2})
+
+    is_odd = lax.rem(seq, 2)
+    before = (seq + last_seq) // n_seq
+    after = (2 * last_seq - seq) // n_seq
+    before2 = (seq + n_seq - 2) // n_seq
+    pl.semaphore_wait(barrier, 3 + before + after + is_odd * (before2 + after))
+
+    pieces = ((0, split), (split, tail_at - split), (tail_at, RIM))
+
+    def piece_copy(step, piece):
+        at, size = pieces[piece]
+        where = tokens.at[pl.ds(me * rows + at, size)]
+        return pltpu.make_async_remote_copy(
+            src_ref=where,
+            dst_ref=where,
+            send_sem=tok_send.at[step, piece],
+            recv_sem=tok_recv.at[step, piece],
+            device_id={"tp": peers[step]},
+            device_id_type=MESH,
+        )
+
+    def relay_copy(half):
+        at, size = pieces[half]
+        there = tokens.at[pl.ds(peers[2 - half] * rows + at, size)]
+        return pltpu.make_async_remote_copy(
+            src_ref=there,
+            dst_ref=there,
+            send_sem=tok_send.at[3, half],
+            recv_sem=tok_recv.at[3, half],
+            device_id={"tp": peers[1 + half]},
+            device_id_type=MESH,
+        )
+
+    def rim_copy():
+        return pltpu.make_async_remote_copy(
+            src_ref=tokens.at[pl.ds(total - RIM, RIM)],
+            dst_ref=rim,
+            send_sem=rim_send,
+            recv_sem=rim_recv,
+            device_id={"seq": seq + 1},
+            device_id_type=MESH,
+        )
+
+    own.wait()
+    for step in (3, 1, 2):
+        piece_copy(step, 2).start()
+    for step, half in ((1, 1), (2, 0), (1, 0), (2, 1)):
+        piece_copy(step, half).start()
+
+    @pl.when(seq == 0)
+    def _():
+        rim[...] = jnp.zeros_like(rim)
+
+    down = lax.broadcasted_iota(jnp.int32, (CHUNK, CHUNK), 0)
+    across = lax.broadcasted_iota(jnp.int32, (CHUNK, CHUNK), 1)
+    eye = low((down == across).astype(jnp.float32))
+    edges = (1, 2, 8, 32, CHUNK)
+    for i in range(4):
+        inside = down // edges[i + 1] == across // edges[i + 1]
+        apart = down // edges[i] != across // edges[i]
+        masks[i] = low(jnp.where(jnp.logical_and(inside, apart), 1.0, 0.0))
+
+    for load in smalls:
+        load.wait()
+    for b in range(3):
+        for i in range(taps):
+            row = conv_ref[b, i : i + 1, :].astype(jnp.float32) * 0.5
+            for h in range(heads):
+                cols = slice(h * dim, (h + 1) * dim)
+                half_taps[b, i, h] = jnp.broadcast_to(row[:, cols], (8, dim))
+    wdb = low(jnp.concatenate([wdb_ref[0].astype(jnp.float32), wdb_ref[1].astype(jnp.float32)], axis=0))
+
+    def project(block, slots, places):
+        def one(b, carry):
+            full = jnp.dot(block, weights[b], preferred_element_type=jnp.float32)
+            full = full.astype(jnp.bfloat16).astype(jnp.float32)
+            for start, size, at in places:
+                for h in range(heads):
+                    proj[b, h, pl.ds(at, size), :] = full[start : start + size, h * dim : (h + 1) * dim]
+            return carry
+
+        lax.fori_loop(slots[0], slots[1], one, 0)
+
+    def project_gate(block, at):
+        full = jnp.dot(block, weights[3], preferred_element_type=jnp.float32)
+        for h in range(heads):
+            gates[h, pl.ds(at, rows), :] = full[:, h * dim : (h + 1) * dim]
+
+    def project_block(slot, slots, gate):
+        at = pl.multiple_of(slot * rows, rows)
+        block = tokens[pl.ds(at, rows), :]
+        project(block, slots, ((0, rows, pl.multiple_of(at + RIM, RIM)),))
+        if gate:
+            project_gate(block, at)
+
+    def half_silu(half):
+        return half + half * jnp.tanh(half)
+
+    def branch(b, h, r0):
+        conv = None
+        for i in range(taps):
+            window = proj[b, h, pl.ds(r0 + (RIM + 1 - taps + i), CHUNK), :]
+            term = window.reshape(CHUNK // 8, 8, dim) * half_taps[order[b], i, h][None]
+            conv = term if conv is None else conv + term
+        return half_silu(conv).astype(jnp.bfloat16).reshape(CHUNK, dim)
+
+    def prepare(c):
+        r0 = pl.multiple_of(c * CHUNK, CHUNK)
+        scalars = lax.dot_general(
+            wdb, tokens[pl.ds(r0, CHUNK), :], NT, preferred_element_type=jnp.float32
+        )
+        for h in range(heads):
+            k = unit_rows(branch(0, h, r0).astype(jnp.float32))
+            v = branch(1, h, r0)
+            u = scalars[h : h + 1, :] + bias_ref[0:1, h : h + 1]
+            log_row = -rate_ref[0:1, h : h + 1] * (jnp.maximum(u, 0.0) + jnp.log1p(jnp.exp(-jnp.abs(u))))
+            rate_row = 1.0 / (1.0 + jnp.exp(-scalars[heads + h : heads + h + 1, :]))
+            cum_col = jnp.sum(jnp.where(across <= down, log_row, 0.0), axis=1, keepdims=True)
+            cum_row = jnp.sum(jnp.where(across == down, cum_col, 0.0), axis=0, keepdims=True)
+            rate_col = jnp.sum(jnp.where(across == down, rate_row, 0.0), axis=1, keepdims=True)
+            end = cum_col[CHUNK - 1 : CHUNK, :]
+            gap = jnp.exp(jnp.where(across <= down, cum_col - cum_row, 0.0))
+            weight = jnp.where(across <= down, gap, 0.0) * rate_row
+            low_k = low(k)
+            lows[c, h] = low(jnp.where(across < down, weight * dot(low_k, low_k, NT), 0.0))
+            run = jnp.exp(cum_col)
+            tail = rate_col * jnp.exp(end - cum_col)
+            rights[c, h] = jnp.concatenate([v, low(k * run)], axis=1)
+            tails[c, h] = low(k * tail)
+            keys[c, h] = low_k
+            decays[c, h] = weight
+            runs[c, h] = jnp.broadcast_to(run, (CHUNK, dim))
+            fades[c, h] = jnp.broadcast_to(jnp.exp(end), (1, dim))
+
+    def solve(chunks):
+        chains = [(c, h) for c in chunks for h in range(heads)]
+        inverse = [eye - lows[c, h] * masks[0] for c, h in chains]
+        for level in (1, 2):
+            step = [low(dot(inverse[i], lows[c, h] * masks[level])) for i, (c, h) in enumerate(chains)]
+            both = [dot(x, jnp.concatenate([low(d), x], axis=1)) for x, d in zip(step, inverse)]
+            first = [d.astype(jnp.float32) - p[:, :CHUNK] for p, d in zip(both, inverse)]
+            inverse = [q + dot(p[:, CHUNK:], q) for p, q in zip(both, first)]
+        both = [
+            dot(inverse[i], jnp.concatenate([lows[c, h] * masks[3], rights[c, h]], axis=1))
+            for i, (c, h) in enumerate(chains)
+        ]
+        again = [dot(p[:, :CHUNK], p) for p in both]
+        first = [p[:, CHUNK:] - a[:, CHUNK:] for p, a in zip(both, again)]
+        for (c, h), a, q in zip(chains, again, first):
+            solves[c, h] = low(q + dot(a[:, :CHUNK], q))
+        for c, h in chains:
+            got = dot(tails[c, h], solves[c, h], TN)
+            maps[c, h] = jnp.concatenate([got[:, :dim], -got[:, dim:]], axis=1)
+
+    def queries(c):
+        r0 = pl.multiple_of(c * CHUNK, CHUNK)
+        for h in range(heads):
+            q = unit_rows(branch(2, h, r0).astype(jnp.float32)) * (1.0 / math.sqrt(dim))
+            attend = decays[c, h] * dot(q, keys[c, h], NT)
+            got = dot(attend, solves[c, h])
+            outs[h, pl.ds(r0, CHUNK), :] = got[:, :dim]
+            qeffs[h, pl.ds(r0, CHUNK), :] = q * runs[c, h] - got[:, dim:]
+
+    loads[0].wait()
+    loads[1].wait()
+    project_block(me, (0, 2), False)
+    loads[2].wait()
+    loads[3].wait()
+    project_block(me, (2, 3), True)
+
+    for step in range(1, 4):
+        piece_copy(step, 2).wait_recv()
+
+    @pl.when(seq < last_seq)
+    def _():
+        rim_copy().start()
+
+    @pl.when(seq > 0)
+    def _():
+        pltpu.make_async_copy(tokens.at[pl.ds(0, RIM)], rim, rim_recv).wait()
+
+    places = [(0, RIM, 0)]
+    edge_rows = [rim[...]]
+    for step in range(1, 4):
+        at = pl.multiple_of(peers[step] * rows + tail_at, RIM)
+        edge_rows.append(tokens[pl.ds(at, RIM), :])
+        places.append((step * RIM, RIM, pl.multiple_of(at + RIM, RIM)))
+    project(jnp.concatenate(edge_rows, axis=0), (0, 3), places)
+
+    prepare(me)
+    piece_copy(1, 1).wait_recv()
+    relay_copy(1).start()
+    piece_copy(2, 0).wait_recv()
+    relay_copy(0).start()
+    solve((me,))
+    queries(me)
+
+    piece_copy(1, 0).wait_recv()
+    project_block(peers[1], (0, 3), True)
+    piece_copy(2, 1).wait_recv()
+    project_block(peers[2], (0, 3), True)
+    prepare(peers[1])
+    prepare(peers[2])
+    solve((peers[1], peers[2]))
+    queries(peers[1])
+    queries(peers[2])
+
+    relay_copy(0).wait_recv()
+    relay_copy(1).wait_recv()
+    project_block(peers[3], (0, 2), False)
+    prepare(peers[3])
+    solve((peers[3],))
+
+    def map_copy(h):
+        return pltpu.make_async_remote_copy(
+            src_ref=map_out.at[h], dst_ref=map_in.at[h], send_sem=map_send.at[h], recv_sem=map_recv.at[h],
+            device_id={"seq": seq + 1}, device_id_type=MESH,
+        )
+
+    def fade_copy():
+        return pltpu.make_async_remote_copy(
+            src_ref=fade_out, dst_ref=fade_in, send_sem=fade_send, recv_sem=fade_recv,
+            device_id={"seq": seq + 1}, device_id_type=MESH,
+        )
+
+    def state_copy(h):
+        return pltpu.make_async_remote_copy(
+            src_ref=st_out.at[h], dst_ref=st_in.at[h], send_sem=st_send.at[h], recv_sem=st_recv.at[h],
+            device_id={"seq": seq + 2}, device_id_type=MESH,
+        )
+
+    def share_copy(h):
+        return pltpu.make_async_remote_copy(
+            src_ref=st_in.at[h], dst_ref=st_in.at[h], send_sem=fw_send.at[h], recv_sem=st_recv.at[h],
+            device_id={"seq": seq - 1}, device_id_type=MESH,
+        )
+
+    for h in range(heads):
+        whole = maps[0, h]
+        fade = fades[0, h]
+        for c in range(1, count):
+            prefixes[c, h] = low(whole)
+            totals[c, h] = fade
+            mine, keep = maps[c, h], fades[c, h]
+            got = dot(mine[:, dim:], whole)
+            left = keep * whole[:, :dim] + mine[:, :dim] + got[:, :dim]
+            right = keep * whole[:, dim:] + fade * mine[:, dim:] + got[:, dim:]
+            whole = jnp.concatenate([left, right], axis=1)
+            fade = keep * fade
+        maps[0, h] = whole
+        map_out[h] = low(whole)
+        fade_out[h] = fade
+
+    @pl.when(even)
+    def _():
+        fade_copy().start()
+        for h in range(heads):
+            map_copy(h).start()
+
+    @pl.when(seq == 0)
+    def _():
+        for h in range(heads):
+            held[h] = jnp.zeros((dim, dim), jnp.bfloat16)
+
+    @pl.when(odd)
+    def _():
+        fade_copy().wait_recv()
+        for h in range(heads):
+            map_copy(h).wait_recv()
+            whole, fade = maps[0, h], fade_out[h]
+            other, its = map_in[h].astype(jnp.float32), fade_in[h]
+            got = dot(whole[:, dim:], map_in[h])
+            base = fade * other[:, :dim] + whole[:, :dim] + got[:, :dim]
+
+            @pl.when(seq == 1)
+            def _():
+                held[h] = map_in[h, :, :dim]
+
+                @pl.when(seq < last_seq)
+                def _():
+                    st_out[h] = low(base)
+                    state_copy(h).start()
+
+            joined_b[h] = base
+            joined[h] = low(fade * other[:, dim:] + its * whole[:, dim:] + got[:, dim:])
+            joined_f[h] = fade * its
+
+    def pass_on():
+        for h in range(heads):
+            state_copy(h).wait_recv()
+            share_copy(h).start()
+            state = st_in[h]
+            wide = state.astype(jnp.float32)
+
+            @pl.when(seq < last_seq)
+            def _():
+                st_out[h] = low(joined_f[h] * wide + joined_b[h] + dot(joined[h], state))
+                state_copy(h).start()
+
+            other = map_in[h]
+            held[h] = low(fade_in[h] * wide + other[:, :dim].astype(jnp.float32) + dot(other[:, dim:], state))
+
+    @pl.when(jnp.logical_and(odd, seq == 3))
+    def _():
+        pass_on()
+
+    project_block(peers[3], (2, 3), True)
+    queries(peers[3])
+    for c in range(count):
+        at = pl.ds(c * CHUNK, CHUNK)
+        for h in range(heads):
+            qeff = qeffs[h, at, :]
+            if c == 0:
+                deltas[h, at, :] = low(qeff)
+            else:
+                got = dot(qeff, prefixes[c, h])
+                outs[h, at, :] = outs[h, at, :] + got[:, :dim]
+                deltas[h, at, :] = low(totals[c, h] * qeff + got[:, dim:])
+
+    @pl.when(jnp.logical_and(odd, seq > 3))
+    def _():
+        pass_on()
+
+    for h in range(heads):
+
+        @pl.when(jnp.logical_and(even, seq > 0))
+        def _():
+            state_copy(h).wait_recv()
+            held[h] = st_in[h]
+
+        cols = slice(h * dim, (h + 1) * dim)
+        read = outs[h] + dot(deltas[h], held[h])
+        scale = lax.rsqrt(jnp.mean(read * read, axis=-1, keepdims=True) + 1e-06)
+        out_ref[:, cols] = low(read * scale * gain_ref[...] * half_silu(0.5 * gates[h]))
+
+    for step in range(1, 4):
+        for piece in range(3):
+            if step == 3 and piece < 2:
+                relay_copy(piece).wait_send()
+            else:
+                piece_copy(step, piece).wait_send()
+
+    @pl.when(seq < last_seq)
+    def _():
+        rim_copy().wait_send()
+
+    @pl.when(even)
+    def _():
+        fade_copy().wait_send()
+        for h in range(heads):
+            map_copy(h).wait_send()
+
+    @pl.when(jnp.logical_and(odd, seq > 1))
+    def _():
+        for h in range(heads):
+            share_copy(h).wait_send()
+
+    @pl.when(jnp.logical_and(odd, seq < last_seq))
+    def _():
+        for h in range(heads):
+            state_copy(h).wait_send()
+
+
+def fast_device(n_seq, hidden, w_qkv, w_gate, w_decay_beta, conv_weight, decay_rate, dt_bias, norm_gain):
+    rows, width = hidden.shape
+    heads = decay_rate.shape[0]
+    dim = norm_gain.shape[0]
+    taps = conv_weight.shape[0]
+    columns = heads * dim
+    total = rows * 4
+    count = total // CHUNK
+    dma = pltpu.SemaphoreType.DMA
+    f32, bf16 = jnp.float32, jnp.bfloat16
+    operands = (
+        decay_rate.reshape(1, heads), dt_bias.reshape(1, heads), hidden,
+        w_qkv.transpose(1, 0, 2), w_gate, w_decay_beta.transpose(1, 2, 0),
+        conv_weight.transpose(1, 0, 2), norm_gain.reshape(1, dim),
+    )
+    return pl.pallas_call(
+        functools.partial(fast_kernel, n_seq),
+        out_shape=jax.ShapeDtypeStruct((total, columns), bf16),
+        in_specs=[pl.BlockSpec(memory_space=pl.ANY)] * 8,
+        out_specs=pl.BlockSpec(memory_space=pltpu.VMEM),
+        scratch_shapes=[
+            pltpu.VMEM((1, heads), f32),
+            pltpu.VMEM((1, heads), f32),
+            pltpu.VMEM((2, heads, width), bf16),
+            pltpu.VMEM((3, taps, columns), bf16),
+            pltpu.VMEM((1, dim), f32),
+            dma((5,)),
+            pltpu.VMEM((total, width), bf16),
+            pltpu.VMEM((RIM, width), bf16),
+            pltpu.VMEM((4, width, columns), bf16),
+            pltpu.VMEM((3, heads, RIM + total, dim), f32),
+            pltpu.VMEM((heads, total, dim), f32),
+            pltpu.VMEM((3, taps, heads, 8, dim), f32),
+            pltpu.VMEM((4, CHUNK, CHUNK), bf16),
+            dma,
+            dma((4, 3)),
+            dma((4, 3)),
+            dma((4,)),
+            dma,
+            dma,
+            pltpu.VMEM((count, heads, CHUNK, CHUNK), bf16),
+            pltpu.VMEM((count, heads, CHUNK, 2 * dim), bf16),
+            pltpu.VMEM((count, heads, CHUNK, dim), bf16),
+            pltpu.VMEM((count, heads, CHUNK, dim), bf16),
+            pltpu.VMEM((count, heads, CHUNK, CHUNK), f32),
+            pltpu.VMEM((count, heads, CHUNK, dim), f32),
+            pltpu.VMEM((count, heads, 1, dim), f32),
+            pltpu.VMEM((count, heads, CHUNK, 2 * dim), bf16),
+            pltpu.VMEM((count, heads, dim, 2 * dim), f32),
+            pltpu.VMEM((count, heads, dim, 2 * dim), bf16),
+            pltpu.VMEM((count, heads, 1, dim), f32),
+            pltpu.VMEM((heads, total, dim), f32),
+            pltpu.VMEM((heads, total, dim), f32),
+            pltpu.VMEM((heads, total, dim), bf16),
+            pltpu.VMEM((heads, dim, 2 * dim), bf16),
+            pltpu.VMEM((heads, dim, 2 * dim), bf16),
+            pltpu.VMEM((heads, 1, dim), f32),
+            pltpu.VMEM((heads, 1, dim), f32),
+            pltpu.VMEM((heads, dim, dim), bf16),
+            pltpu.VMEM((heads, dim, dim), f32),
+            pltpu.VMEM((heads, 1, dim), f32),
+            dma((heads,)),
+            dma((heads,)),
+            dma,
+            dma,
+            pltpu.VMEM((heads, dim, dim), bf16),
+            pltpu.VMEM((heads, dim, dim), bf16),
+            pltpu.VMEM((heads, dim, dim), bf16),
+            dma((heads,)),
+            dma((heads,)),
+            dma((heads,)),
+        ],
+        compiler_params=pltpu.CompilerParams(
+            collective_id=0, has_side_effects=True, vmem_limit_bytes=48 * 1024 * 1024
+        ),
+    )(*[pltpu.with_memory_space_constraint(x, pltpu.HBM) for x in operands])
+
+
+def per_device(n_seq, n_tp, hidden, *rest):
+    if n_tp == 4 and hidden.shape[0] == CHUNK and n_seq % 2 == 0:
+        return fast_device(n_seq, hidden, *rest)
+    return plain_device(n_seq, n_tp, hidden, *rest)
+
+
 def solution(mesh):
     return jax.shard_map(
         functools.partial(per_device, mesh.shape["seq"], mesh.shape["tp"]),

time: 49.7 us -> 41.1 us (0.83)
  Pallas kernels: 47.7 us -> 40.2 us
  local copies, waits for them, and re-layouts: 1.87 us -> 0.8 us
    pallas_call x1, Pallas kernels: 47.7 us -> 40.2 us  [fast_device(): pl.pallas_call(functools.partial(fast_kernel, n_seq), out_shape=jax.Shape...]
    unnamed x1, local copies, waits for them, and re-layouts: 1.87 us -> 0.8 us
where the time goes in v1:
time: 41.1 us; the launch traced here: 41 us
  Pallas kernels  40.2 us (98%)
  local copies, waits for them, and re-layouts  0.8 us (2%)
    pallas_call x1, Pallas kernels, fast_device(): pl.pallas_call(functools.partial(fast_kernel, n_seq), out_shape=jax.Shape...  40.2 us

profile of v1, /device:TPU:25, one launch (start us, length us, event | category | flops | bytes accessed | tf_op | source)
XLA Modules:
  0.0 41.0 jit_solution(3597920015018887850)
XLA Ops:
  0.0 40.2 %shard_map.82 = bf16[512,512]{1,0:T(8,128)(2,1)S(1)} custom-call(f32[1,4]{1,0:T(1,128)} %bitcast.9, f32[1,4]{1,0:T(1,128)} %bitcast.10, bf16[128,2048]{1,0:T(8,128)(2,1)} %hidden.1, bf16[3,2048,512]{2,1,0:T(8,128)(2,1)} %bitcast.6, bf16[2048,512]{1,0:T(8,128)(2,1)} %w_gate.1, bf16[2,4,2048]{2,1,0:T(4,128)(2,1)} %bitcast.7, bf16[3,4,512]{2,1,0:T(4,128)(2,1)} %bitcast.8, ...), custom_call_target="tpu_custom_call" | custom-call | tf_op jit(solution)/shard_map/pallas_call | solution.py:859
  40.2 0.8 %copy.10 = bf16[512,512]{1,0:T(8,128)(2,1)} copy(bf16[512,512]{1,0:T(8,128)(2,1)S(1)} %shard_map.82) | data formatting | bytes 1048576

commit v2 on v1

--- a/solution.py
+++ b/solution.py
@@ -424,12 +424,12 @@
 def fast_kernel(
     n_seq, rate_hbm, bias_hbm, hidden, w_qkv, w_gate, wdb_hbm, conv_hbm, gain_hbm, out_ref,
     rate_ref, bias_ref, wdb_ref, conv_ref, gain_ref, small_sem,
-    tokens, rim, weights, proj, gates, half_taps, masks,
+    tokens, rim, weights, proj_k, proj_v, proj_q, gates, half_taps, masks,
     own_sem, tok_send, tok_recv, w_sem, rim_send, rim_recv,
-    lows, rights, keys, tails, decays, runs, fades, solves, maps, prefixes, totals, qeffs, outs, deltas,
-    map_out, map_in, fade_out, fade_in, joined, joined_b, joined_f,
-    map_send, map_recv, fade_send, fade_recv,
-    st_in, st_out, held, st_send, st_recv, fw_send,
+    betas, keys, decays, runs, fades, solves, maps, pairs, pair_fades, qeffs, outs, deltas,
+    map_out, map_in, fade_out, fade_in, joined, joined_b, joined_f, far_in, far_fade,
+    map_send, map_recv, fade_send, fade_recv, far_send, far_recv, far_fade_send, far_fade_recv,
+    st_in, st_out, held, st_send, st_recv, fw_send, skip_send,
 ):
     seq, me = lax.axis_index("seq"), lax.axis_index("tp")
     last_seq = n_seq - 1
@@ -441,7 +441,8 @@
     dim = gain_ref.shape[1]
     taps = conv_ref.shape[1]
     count = total // CHUNK
-    split = 48
+    half_rows = rows // 2
+    proj = (proj_k, proj_v, proj_q)
     tail_at = rows - RIM
 
     own = pltpu.make_async_copy(hidden, tokens.at[pl.ds(me * rows, rows)], own_sem)
@@ -451,7 +452,7 @@
     loads.append(pltpu.make_async_copy(w_gate, weights.at[3], w_sem.at[3]))
     small = [(rate_hbm, rate_ref), (bias_hbm, bias_ref), (wdb_hbm, wdb_ref), (conv_hbm, conv_ref), (gain_hbm, gain_ref)]
     smalls = [pltpu.make_async_copy(src, dst, small_sem.at[i]) for i, (src, dst) in enumerate(small)]
-    for load in loads + smalls:
+    for load in smalls:
         load.start()
 
     barrier = pltpu.get_barrier_semaphore()
@@ -460,7 +461,7 @@
         pl.semaphore_signal(barrier, inc=1, device_id=where, device_id_type=MESH)
 
     peers = [peer_of(me, step, 4) for step in range(4)]
-    for step in range(1, 4):
+    for step in range(1, 3):
         greet({"tp": peers[step]})
 
     @pl.when(seq > 0)
@@ -478,14 +479,24 @@
     @pl.when(jnp.logical_and(odd, seq < last_seq))
     def _():
         greet({"seq": seq + 2})
+
+    @pl.when(seq == last_seq)
+    def _():
+        greet({"seq": last_seq - 4})
+
+    @pl.when(seq == last_seq - 4)
+    def _():
+        greet({"seq": last_seq})
 
     is_odd = lax.rem(seq, 2)
     before = (seq + last_seq) // n_seq
     after = (2 * last_seq - seq) // n_seq
     before2 = (seq + n_seq - 2) // n_seq
-    pl.semaphore_wait(barrier, 3 + before + after + is_odd * (before2 + after))
-
-    pieces = ((0, split), (split, tail_at - split), (tail_at, RIM))
+    skips = seq // last_seq + ((seq + 1) // (last_seq - 3)) * ((last_seq - 3) // (seq + 1))
+    pl.semaphore_wait(barrier, 2 + before + after + is_odd * (before2 + after) + skips)
+
+    quarter = half_rows // 2
+    pieces = ((0, quarter), (quarter, quarter), (half_rows, tail_at - half_rows), (tail_at, RIM))
 
     def piece_copy(step, piece):
         at, size = pieces[piece]
@@ -499,15 +510,16 @@
             device_id_type=MESH,
         )
 
-    def relay_copy(half):
-        at, size = pieces[half]
-        there = tokens.at[pl.ds(peers[2 - half] * rows + at, size)]
+    def relay_copy(piece):
+        at, size = pieces[piece]
+        via = 1 if piece < 2 else 2
+        there = tokens.at[pl.ds(peers[3 - via] * rows + at, size)]
         return pltpu.make_async_remote_copy(
             src_ref=there,
             dst_ref=there,
-            send_sem=tok_send.at[3, half],
-            recv_sem=tok_recv.at[3, half],
-            device_id={"tp": peers[1 + half]},
+            send_sem=tok_send.at[3, piece],
+            recv_sem=tok_recv.at[3, piece],
+            device_id={"tp": peers[via]},
             device_id_type=MESH,
         )
 
@@ -522,10 +534,10 @@
         )
 
     own.wait()
-    for step in (3, 1, 2):
-        piece_copy(step, 2).start()
-    for step, half in ((1, 1), (2, 0), (1, 0), (2, 1)):
-        piece_copy(step, half).start()
+    for step, piece in ((1, 3), (2, 3), (1, 2), (2, 0)):
+        piece_copy(step, piece).start()
+    for load in loads:
+        load.start()
 
     @pl.when(seq == 0)
     def _():
@@ -550,28 +562,27 @@
                 half_taps[b, i, h] = jnp.broadcast_to(row[:, cols], (8, dim))
     wdb = low(jnp.concatenate([wdb_ref[0].astype(jnp.float32), wdb_ref[1].astype(jnp.float32)], axis=0))
 
-    def project(block, slots, places):
-        def one(b, carry):
+    def project(block, branches, places):
+        for b in branches:
             full = jnp.dot(block, weights[b], preferred_element_type=jnp.float32)
-            full = full.astype(jnp.bfloat16).astype(jnp.float32)
-            for start, size, at in places:
+            if b < 3:
+                full = full.astype(jnp.bfloat16).astype(jnp.float32)
+            for start, size, at, edge in places:
                 for h in range(heads):
-                    proj[b, h, pl.ds(at, size), :] = full[start : start + size, h * dim : (h + 1) * dim]
-            return carry
-
-        lax.fori_loop(slots[0], slots[1], one, 0)
-
-    def project_gate(block, at):
-        full = jnp.dot(block, weights[3], preferred_element_type=jnp.float32)
-        for h in range(heads):
-            gates[h, pl.ds(at, rows), :] = full[:, h * dim : (h + 1) * dim]
-
-    def project_block(slot, slots, gate):
-        at = pl.multiple_of(slot * rows, rows)
-        block = tokens[pl.ds(at, rows), :]
-        project(block, slots, ((0, rows, pl.multiple_of(at + RIM, RIM)),))
-        if gate:
-            project_gate(block, at)
+                    got = full[start : start + size, h * dim : (h + 1) * dim]
+                    if b < 3:
+                        proj[b][h, pl.ds(pl.multiple_of(at + RIM, RIM), size), :] = got
+                    elif not edge:
+                        gates[h, pl.ds(pl.multiple_of(at, RIM), size), :] = got
+
+    def take(runs_of_rows):
+        blocks, places, start = [], [], 0
+        for slot, at, size in runs_of_rows:
+            begin = pl.multiple_of(slot * rows + at, RIM)
+            blocks.append(tokens[pl.ds(begin, size), :])
+            places.append((start, size, begin, size == RIM))
+            start += size
+        return jnp.concatenate(blocks, axis=0), places
 
     def half_silu(half):
         return half + half * jnp.tanh(half)
@@ -579,19 +590,17 @@
     def branch(b, h, r0):
         conv = None
         for i in range(taps):
-            window = proj[b, h, pl.ds(r0 + (RIM + 1 - taps + i), CHUNK), :]
+            window = proj[b][h, pl.ds(r0 + (RIM + 1 - taps + i), CHUNK), :]
             term = window.reshape(CHUNK // 8, 8, dim) * half_taps[order[b], i, h][None]
             conv = term if conv is None else conv + term
         return half_silu(conv).astype(jnp.bfloat16).reshape(CHUNK, dim)
 
-    def prepare(c):
+    def gate_rows(c):
         r0 = pl.multiple_of(c * CHUNK, CHUNK)
         scalars = lax.dot_general(
             wdb, tokens[pl.ds(r0, CHUNK), :], NT, preferred_element_type=jnp.float32
         )
         for h in range(heads):
-            k = unit_rows(branch(0, h, r0).astype(jnp.float32))
-            v = branch(1, h, r0)
             u = scalars[h : h + 1, :] + bias_ref[0:1, h : h + 1]
             log_row = -rate_ref[0:1, h : h + 1] * (jnp.maximum(u, 0.0) + jnp.log1p(jnp.exp(-jnp.abs(u))))
             rate_row = 1.0 / (1.0 + jnp.exp(-scalars[heads + h : heads + h + 1, :]))
@@ -600,36 +609,40 @@
             rate_col = jnp.sum(jnp.where(across == down, rate_row, 0.0), axis=1, keepdims=True)
             end = cum_col[CHUNK - 1 : CHUNK, :]
             gap = jnp.exp(jnp.where(across <= down, cum_col - cum_row, 0.0))
-            weight = jnp.where(across <= down, gap, 0.0) * rate_row
+            decays[c, h] = jnp.where(across <= down, gap, 0.0) * rate_row
+            runs[c, h] = jnp.broadcast_to(jnp.exp(cum_col), (CHUNK, dim))
+            betas[c, h] = jnp.broadcast_to(rate_col * jnp.exp(end - cum_col), (CHUNK, dim))
+            fades[c, h] = jnp.broadcast_to(jnp.exp(end), (1, dim))
+
+    def prepare(c):
+        r0 = pl.multiple_of(c * CHUNK, CHUNK)
+        chains = []
+        for h in range(heads):
+            k = unit_rows(branch(0, h, r0).astype(jnp.float32))
             low_k = low(k)
-            lows[c, h] = low(jnp.where(across < down, weight * dot(low_k, low_k, NT), 0.0))
-            run = jnp.exp(cum_col)
-            tail = rate_col * jnp.exp(end - cum_col)
-            rights[c, h] = jnp.concatenate([v, low(k * run)], axis=1)
-            tails[c, h] = low(k * tail)
             keys[c, h] = low_k
-            decays[c, h] = weight
-            runs[c, h] = jnp.broadcast_to(run, (CHUNK, dim))
-            fades[c, h] = jnp.broadcast_to(jnp.exp(end), (1, dim))
-
-    def solve(chunks):
-        chains = [(c, h) for c in chunks for h in range(heads)]
-        inverse = [eye - lows[c, h] * masks[0] for c, h in chains]
+            mixing = low(jnp.where(across < down, decays[c, h] * dot(low_k, low_k, NT), 0.0))
+            chains.append((c, h, mixing, low(k * runs[c, h]), low(k * betas[c, h]), branch(1, h, r0)))
+        return chains
+
+    def solve(chains):
+        inverse = [eye - mixing * masks[0] for _, _, mixing, _, _, _ in chains]
         for level in (1, 2):
-            step = [low(dot(inverse[i], lows[c, h] * masks[level])) for i, (c, h) in enumerate(chains)]
+            step = [low(dot(d, item[2] * masks[level])) for d, item in zip(inverse, chains)]
             both = [dot(x, jnp.concatenate([low(d), x], axis=1)) for x, d in zip(step, inverse)]
             first = [d.astype(jnp.float32) - p[:, :CHUNK] for p, d in zip(both, inverse)]
             inverse = [q + dot(p[:, CHUNK:], q) for p, q in zip(both, first)]
         both = [
-            dot(inverse[i], jnp.concatenate([lows[c, h] * masks[3], rights[c, h]], axis=1))
-            for i, (c, h) in enumerate(chains)
+            dot(d, jnp.concatenate([mixing * masks[3], v, k_run], axis=1))
+            for d, (_, _, mixing, k_run, _, v) in zip(inverse, chains)
         ]
         again = [dot(p[:, :CHUNK], p) for p in both]
         first = [p[:, CHUNK:] - a[:, CHUNK:] for p, a in zip(both, again)]
-        for (c, h), a, q in zip(chains, again, first):
-            solves[c, h] = low(q + dot(a[:, :CHUNK], q))
-        for c, h in chains:
-            got = dot(tails[c, h], solves[c, h], TN)
+        solved = [low(q + dot(a[:, :CHUNK], q)) for a, q in zip(again, first)]
+        for item, value in zip(chains, solved):
+            c, h = item[:2]
+            solves[c, h] = value
+            got = dot(item[4], value, TN)
             maps[c, h] = jnp.concatenate([got[:, :dim], -got[:, dim:]], axis=1)
 
     def queries(c):
@@ -641,165 +654,258 @@
             outs[h, pl.ds(r0, CHUNK), :] = got[:, :dim]
             qeffs[h, pl.ds(r0, CHUNK), :] = q * runs[c, h] - got[:, dim:]
 
-    loads[0].wait()
-    loads[1].wait()
-    project_block(me, (0, 2), False)
-    loads[2].wait()
-    loads[3].wait()
-    project_block(me, (2, 3), True)
-
-    for step in range(1, 4):
-        piece_copy(step, 2).wait_recv()
+    def join(late, early):
+        (high, keep), (whole, fade) = late, early
+        got = dot(high[:, dim:], whole)
+        left = keep * whole[:, :dim] + high[:, :dim] + got[:, :dim]
+        right = keep * whole[:, dim:] + fade * high[:, dim:] + got[:, dim:]
+        return jnp.concatenate([left, right], axis=1), keep * fade
+
+    def pair_up(p):
+        for h in range(heads):
+            whole, fade = join((maps[2 * p + 1, h], fades[2 * p + 1, h]), (maps[2 * p, h], fades[2 * p, h]))
+            pairs[p, h] = whole
+            pair_fades[p, h] = fade
+
+    piece_copy(1, 3).wait_recv()
+    relay_copy(3).start()
+    for step, piece in ((1, 0), (1, 1), (2, 1), (2, 2)):
+        piece_copy(step, piece).start()
+
+    for load in loads:
+        load.wait()
+    block, places = take(((me, 0, rows),))
+    project(block, range(4), places)
+
+    piece_copy(2, 3).wait_recv()
+    relay_copy(3).wait_recv()
 
     @pl.when(seq < last_seq)
     def _():
         rim_copy().start()
 
-    @pl.when(seq > 0)
-    def _():
-        pltpu.make_async_copy(tokens.at[pl.ds(0, RIM)], rim, rim_recv).wait()
-
-    places = [(0, RIM, 0)]
-    edge_rows = [rim[...]]
-    for step in range(1, 4):
-        at = pl.multiple_of(peers[step] * rows + tail_at, RIM)
-        edge_rows.append(tokens[pl.ds(at, RIM), :])
-        places.append((step * RIM, RIM, pl.multiple_of(at + RIM, RIM)))
-    project(jnp.concatenate(edge_rows, axis=0), (0, 3), places)
-
-    prepare(me)
-    piece_copy(1, 1).wait_recv()
-    relay_copy(1).start()
+    piece_copy(1, 2).wait_recv()
+    relay_copy(2).start()
     piece_copy(2, 0).wait_recv()
     relay_copy(0).start()
-    solve((me,))
+
+    @pl.when(seq > 0)
+    def _():
+        pltpu.make_async_copy(tokens.at[pl.ds(0, RIM)], rim, rim_recv).wait()
+
+    block, places = take(((peers[1], half_rows, half_rows), (peers[2], 0, quarter), (peers[3], tail_at, RIM)))
+    block = jnp.concatenate([block, rim[...]], axis=0)
+    project(block, range(4), places + [(rows - RIM, RIM, -RIM, True)])
+    piece_copy(2, 1).wait_recv()
+    relay_copy(1).start()
+    gate_rows(me)
+    solve(prepare(me))
     queries(me)
 
     piece_copy(1, 0).wait_recv()
-    project_block(peers[1], (0, 3), True)
-    piece_copy(2, 1).wait_recv()
-    project_block(peers[2], (0, 3), True)
-    prepare(peers[1])
-    prepare(peers[2])
-    solve((peers[1], peers[2]))
+    piece_copy(1, 1).wait_recv()
+    piece_copy(2, 2).wait_recv()
+    late, late_places = take(((peers[1], 0, half_rows), (peers[2], quarter, rows - quarter)))
+    gate_rows(peers[1])
+    gate_rows(peers[2])
+    project(late, range(2), late_places)
+    solve(prepare(peers[1]) + prepare(peers[2]))
+    pair_up(me // 2)
+
+    for piece in range(3):
+        relay_copy(piece).wait_recv()
+    block, places = take(((peers[3], 0, rows),))
+    gate_rows(peers[3])
+    project(block, range(2), places)
+    solve(prepare(peers[3]))
+    pair_up(1 - me // 2)
+
+    def map_copy(h):
+        return pltpu.make_async_remote_copy(
+            src_ref=map_out.at[h], dst_ref=map_in.at[h], send_sem=map_send.at[h], recv_sem=map_recv.at[h],
+            device_id={"seq": seq + 1}, device_id_type=MESH,
+        )
+
+    def fade_copy():
+        return pltpu.make_async_remote_copy(
+            src_ref=fade_out, dst_ref=fade_in, send_sem=fade_send, recv_sem=fade_recv,
+            device_id={"seq": seq + 1}, device_id_type=MESH,
+        )
+
+    def state_copy(h):
+        return pltpu.make_async_remote_copy(
+            src_ref=st_out.at[h], dst_ref=st_in.at[h], send_sem=st_send.at[h], recv_sem=st_recv.at[h],
+            device_id={"seq": seq + 2}, device_id_type=MESH,
+        )
+
+    def skip_copy(h):
+        return pltpu.make_async_remote_copy(
+            src_ref=st_out.at[h], dst_ref=st_in.at[h], send_sem=skip_send.at[h], recv_sem=st_recv.at[h],
+            device_id={"seq": seq + 4}, device_id_type=MESH,
+        )
+
+    def far_copy(h):
+        return pltpu.make_async_remote_copy(
+            src_ref=map_out.at[h], dst_ref=far_in.at[h], send_sem=far_send.at[h], recv_sem=far_recv.at[h],
+            device_id={"seq": seq + 2}, device_id_type=MESH,
+        )
+
+    def far_fade_copy():
+        return pltpu.make_async_remote_copy(
+            src_ref=joined_f, dst_ref=far_fade, send_sem=far_fade_send, recv_sem=far_fade_recv,
+            device_id={"seq": seq + 2}, device_id_type=MESH,
+        )
+
+    def share_copy(h, source):
+        return pltpu.make_async_remote_copy(
+            src_ref=source.at[h], dst_ref=st_in.at[h], send_sem=fw_send.at[h], recv_sem=st_recv.at[h],
+            device_id={"seq": seq - 1}, device_id_type=MESH,
+        )
+
+    @pl.when(even)
+    def _():
+        for h in range(heads):
+            whole, fade = join((pairs[1, h], pair_fades[1, h]), (pairs[0, h], pair_fades[0, h]))
+            map_out[h] = low(whole)
+            fade_out[h] = fade
+            map_copy(h).start()
+        fade_copy().start()
+
+    @pl.when(seq == 0)
+    def _():
+        for h in range(heads):
+            held[h] = jnp.zeros((dim, dim), jnp.bfloat16)
+
+    def send_on(skip):
+        def send(h):
+            if skip:
+                skip_copy(h).start()
+            else:
+                state_copy(h).start()
+
+        return send
+
+    def whole_map(h):
+        return join((pairs[1, h], pair_fades[1, h]), (pairs[0, h], pair_fades[0, h]))
+
+    def sent_map(h):
+        return map_in[h].astype(jnp.float32), fade_in[h]
+
+    def begin(skip):
+        mine = [whole_map(h) for h in range(heads)]
+        fade_copy().wait_recv()
+        for h in range(heads):
+            map_copy(h).wait_recv()
+            (whole, fade), state = mine[h], map_in[h, :, :dim]
+            base = fade * state.astype(jnp.float32) + whole[:, :dim]
+            st_out[h] = low(base + dot(whole[:, dim:], state))
+            send_on(skip)(h)
+        for h in range(heads):
+            held[h] = map_in[h, :, :dim]
+            if skip:
+                state_copy(h).start()
+
+    def compose():
+        mine = [whole_map(h) for h in range(heads)]
+        fade_copy().wait_recv()
+        for h in range(heads):
+            map_copy(h).wait_recv()
+        both = [join(mine[h], sent_map(h)) for h in range(heads)]
+        for h, (whole, fade) in enumerate(both):
+            joined_b[h] = whole[:, :dim]
+            joined[h] = whole[:, dim:]
+            joined_f[h] = fade
+            map_out[h] = low(whole)
+
+        @pl.when(seq == last_seq - 2)
+        def _():
+            for h in range(heads):
+                far_copy(h).start()
+            far_fade_copy().start()
+
+    @pl.when(seq == 1)
+    def _():
+        begin(last_seq == 5)
+
+    @pl.when(jnp.logical_and(jnp.logical_and(odd, seq > 1), seq < last_seq))
+    def _():
+        compose()
+
+    def carry(h, state, whole, fade):
+        wide = state.astype(jnp.float32)
+        return low(fade * wide + whole[:, :dim].astype(jnp.float32) + dot(whole[:, dim:], state))
+
+    def pass_on(more, skip):
+        for h in range(heads):
+            state_copy(h).wait_recv()
+            if more:
+                state = st_in[h]
+                wide = joined_f[h] * state.astype(jnp.float32) + joined_b[h]
+                st_out[h] = low(wide + dot(joined[h], state))
+                send_on(skip)(h)
+            share_copy(h, st_in).start()
+        for h in range(heads):
+            if more and skip:
+                state_copy(h).start()
+            held[h] = carry(h, st_in[h], map_in[h], fade_in[h])
+
+    def end_chain():
+        fade_copy().wait_recv()
+        far_fade_copy().wait_recv()
+        for h in range(heads):
+            map_copy(h).wait_recv()
+            far_copy(h).wait_recv()
+        for h in range(heads):
+            whole, fade = join(sent_map(h), (far_in[h].astype(jnp.float32), far_fade[h]))
+            joined_b[h] = whole[:, :dim]
+            joined[h] = whole[:, dim:]
+            joined_f[h] = fade
+        for h in range(heads):
+            state_copy(h).wait_recv()
+            state = st_in[h]
+            st_out[h] = carry(h, state, far_in[h], far_fade[h])
+            share_copy(h, st_out).start()
+            wide = joined_f[h] * state.astype(jnp.float32) + joined_b[h]
+            held[h] = low(wide + dot(joined[h], state))
+
+    project(late, range(2, 4), late_places)
     queries(peers[1])
     queries(peers[2])
 
-    relay_copy(0).wait_recv()
-    relay_copy(1).wait_recv()
-    project_block(peers[3], (0, 2), False)
-    prepare(peers[3])
-    solve((peers[3],))
-
-    def map_copy(h):
-        return pltpu.make_async_remote_copy(
-            src_ref=map_out.at[h], dst_ref=map_in.at[h], send_sem=map_send.at[h], recv_sem=map_recv.at[h],
-            device_id={"seq": seq + 1}, device_id_type=MESH,
-        )
-
-    def fade_copy():
-        return pltpu.make_async_remote_copy(
-            src_ref=fade_out, dst_ref=fade_in, send_sem=fade_send, recv_sem=fade_recv,
-            device_id={"seq": seq + 1}, device_id_type=MESH,
-        )
-
-    def state_copy(h):
-        return pltpu.make_async_remote_copy(
-            src_ref=st_out.at[h], dst_ref=st_in.at[h], send_sem=st_send.at[h], recv_sem=st_recv.at[h],
-            device_id={"seq": seq + 2}, device_id_type=MESH,
-        )
-
-    def share_copy(h):
-        return pltpu.make_async_remote_copy(
-            src_ref=st_in.at[h], dst_ref=st_in.at[h], send_sem=fw_send.at[h], recv_sem=st_recv.at[h],
-            device_id={"seq": seq - 1}, device_id_type=MESH,
-        )
-
+    @pl.when(jnp.logical_and(jnp.logical_and(odd, seq > 1), seq < last_seq - 4))
+    def _():
+        pass_on(True, False)
+
+    if last_seq > 5:
+
+        @pl.when(seq == last_seq - 4)
+        def _():
+            pass_on(True, True)
+
+    project(block, range(2, 4), places)
+    queries(peers[3])
     for h in range(heads):
-        whole = maps[0, h]
-        fade = fades[0, h]
-        for c in range(1, count):
-            prefixes[c, h] = low(whole)
-            totals[c, h] = fade
-            mine, keep = maps[c, h], fades[c, h]
-            got = dot(mine[:, dim:], whole)
-            left = keep * whole[:, :dim] + mine[:, :dim] + got[:, :dim]
-            right = keep * whole[:, dim:] + fade * mine[:, dim:] + got[:, dim:]
-            whole = jnp.concatenate([left, right], axis=1)
-            fade = keep * fade
-        maps[0, h] = whole
-        map_out[h] = low(whole)
-        fade_out[h] = fade
-
-    @pl.when(even)
-    def _():
-        fade_copy().start()
-        for h in range(heads):
-            map_copy(h).start()
-
-    @pl.when(seq == 0)
-    def _():
-        for h in range(heads):
-            held[h] = jnp.zeros((dim, dim), jnp.bfloat16)
-
-    @pl.when(odd)
-    def _():
-        fade_copy().wait_recv()
-        for h in range(heads):
-            map_copy(h).wait_recv()
-            whole, fade = maps[0, h], fade_out[h]
-            other, its = map_in[h].astype(jnp.float32), fade_in[h]
-            got = dot(whole[:, dim:], map_in[h])
-            base = fade * other[:, :dim] + whole[:, :dim] + got[:, :dim]
-
-            @pl.when(seq == 1)
-            def _():
-                held[h] = map_in[h, :, :dim]
-
-                @pl.when(seq < last_seq)
-                def _():
-                    st_out[h] = low(base)
-                    state_copy(h).start()
-
-            joined_b[h] = base
-            joined[h] = low(fade * other[:, dim:] + its * whole[:, dim:] + got[:, dim:])
-            joined_f[h] = fade * its
-
-    def pass_on():
-        for h in range(heads):
-            state_copy(h).wait_recv()
-            share_copy(h).start()
-            state = st_in[h]
-            wide = state.astype(jnp.float32)
-
-            @pl.when(seq < last_seq)
-            def _():
-                st_out[h] = low(joined_f[h] * wide + joined_b[h] + dot(joined[h], state))
-                state_copy(h).start()
-
-            other = map_in[h]
-            held[h] = low(fade_in[h] * wide + other[:, :dim].astype(jnp.float32) + dot(other[:, dim:], state))
-
-    @pl.when(jnp.logical_and(odd, seq == 3))
-    def _():
-        pass_on()
-
-    project_block(peers[3], (2, 3), True)
-    queries(peers[3])
-    for c in range(count):
-        at = pl.ds(c * CHUNK, CHUNK)
-        for h in range(heads):
+        third, fade = join((maps[2, h], fades[2, h]), (pairs[0, h], pair_fades[0, h]))
+        for c in range(count):
+            at = pl.ds(c * CHUNK, CHUNK)
             qeff = qeffs[h, at, :]
             if c == 0:
                 deltas[h, at, :] = low(qeff)
             else:
-                got = dot(qeff, prefixes[c, h])
+                prefix, keep = (
+                    (maps[0, h], fades[0, h]), (pairs[0, h], pair_fades[0, h]), (third, fade)
+                )[c - 1]
+                got = dot(qeff, prefix)
                 outs[h, at, :] = outs[h, at, :] + got[:, :dim]
-                deltas[h, at, :] = low(totals[c, h] * qeff + got[:, dim:])
-
-    @pl.when(jnp.logical_and(odd, seq > 3))
-    def _():
-        pass_on()
+                deltas[h, at, :] = low(keep * qeff + got[:, dim:])
+
+    @pl.when(seq == last_seq - 2)
+    def _():
+        pass_on(False, False)
+
+    @pl.when(seq == last_seq)
+    def _():
+        end_chain()
 
     for h in range(heads):
 
@@ -814,8 +920,8 @@
         out_ref[:, cols] = low(read * scale * gain_ref[...] * half_silu(0.5 * gates[h]))
 
     for step in range(1, 4):
-        for piece in range(3):
-            if step == 3 and piece < 2:
+        for piece in range(4):
+            if step == 3:
                 relay_copy(piece).wait_send()
             else:
                 piece_copy(step, piece).wait_send()
@@ -833,12 +939,23 @@
     @pl.when(jnp.logical_and(odd, seq > 1))
     def _():
         for h in range(heads):
-            share_copy(h).wait_send()
-
-    @pl.when(jnp.logical_and(odd, seq < last_seq))
+            share_copy(h, st_in).wait_send()
+
+    @pl.when(jnp.logical_and(odd, seq <= last_seq - 4))
     def _():
         for h in range(heads):
             state_copy(h).wait_send()
+
+    @pl.when(seq == last_seq - 4)
+    def _():
+        for h in range(heads):
+            skip_copy(h).wait_send()
+
+    @pl.when(seq == last_seq - 2)
+    def _():
+        far_fade_copy().wait_send()
+        for h in range(heads):
+            far_copy(h).wait_send()
 
 
 def fast_device(n_seq, hidden, w_qkv, w_gate, w_decay_beta, conv_weight, decay_rate, dt_bias, norm_gain):
@@ -871,27 +988,27 @@
             pltpu.VMEM((total, width), bf16),
             pltpu.VMEM((RIM, width), bf16),
             pltpu.VMEM((4, width, columns), bf16),
-            pltpu.VMEM((3, heads, RIM + total, dim), f32),
+            pltpu.VMEM((heads, RIM + total, dim), f32),
+            pltpu.VMEM((heads, RIM + total, dim), f32),
+            pltpu.VMEM((heads, RIM + total, dim), f32),
             pltpu.VMEM((heads, total, dim), f32),
             pltpu.VMEM((3, taps, heads, 8, dim), f32),
             pltpu.VMEM((4, CHUNK, CHUNK), bf16),
             dma,
-            dma((4, 3)),
-            dma((4, 3)),
+            dma((4, 4)),
+            dma((4, 4)),
             dma((4,)),
             dma,
             dma,
-            pltpu.VMEM((count, heads, CHUNK, CHUNK), bf16),
-            pltpu.VMEM((count, heads, CHUNK, 2 * dim), bf16),
-            pltpu.VMEM((count, heads, CHUNK, dim), bf16),
+            pltpu.VMEM((count, heads, CHUNK, dim), f32),
             pltpu.VMEM((count, heads, CHUNK, dim), bf16),
             pltpu.VMEM((count, heads, CHUNK, CHUNK), f32),
             pltpu.VMEM((count, heads, CHUNK, dim), f32),
             pltpu.VMEM((count, heads, 1, dim), f32),
             pltpu.VMEM((count, heads, CHUNK, 2 * dim), bf16),
             pltpu.VMEM((count, heads, dim, 2 * dim), f32),
-            pltpu.VMEM((count, heads, dim, 2 * dim), bf16),
-            pltpu.VMEM((count, heads, 1, dim), f32),
+            pltpu.VMEM((2, heads, dim, 2 * dim), f32),
+            pltpu.VMEM((2, heads, 1, dim), f32),
             pltpu.VMEM((heads, total, dim), f32),
             pltpu.VMEM((heads, total, dim), f32),
             pltpu.VMEM((heads, total, dim), bf16),
@@ -899,9 +1016,15 @@
             pltpu.VMEM((heads, dim, 2 * dim), bf16),
             pltpu.VMEM((heads, 1, dim), f32),
             pltpu.VMEM((heads, 1, dim), f32),
-            pltpu.VMEM((heads, dim, dim), bf16),
+            pltpu.VMEM((heads, dim, dim), f32),
             pltpu.VMEM((heads, dim, dim), f32),
             pltpu.VMEM((heads, 1, dim), f32),
+            pltpu.VMEM((heads, dim, 2 * dim), bf16),
+            pltpu.VMEM((heads, 1, dim), f32),
+            dma((heads,)),
+            dma((heads,)),
+            dma,
+            dma,
             dma((heads,)),
             dma((heads,)),
             dma,
@@ -912,6 +1035,7 @@
             dma((heads,)),
             dma((heads,)),
             dma((heads,)),
+            dma((heads,)),
         ],
         compiler_params=pltpu.CompilerParams(
             collective_id=0, has_side_effects=True, vmem_limit_bytes=48 * 1024 * 1024
@@ -920,7 +1044,7 @@
 
 
 def per_device(n_seq, n_tp, hidden, *rest):
-    if n_tp == 4 and hidden.shape[0] == CHUNK and n_seq % 2 == 0:
+    if n_tp == 4 and hidden.shape[0] == CHUNK and n_seq % 2 == 0 and n_seq >= 6:
         return fast_device(n_seq, hidden, *rest)
     return plain_device(n_seq, n_tp, hidden, *rest)
 

time: 41.1 us -> 35.8 us (0.87)
  Pallas kernels: 40.2 us -> 34.9 us
    pallas_call x1, Pallas kernels: 40.2 us -> 34.9 us  [fast_device(): pl.pallas_call(functools.partial(fast_kernel, n_seq), out_shape=jax.Shape...]
where the time goes in v2:
time: 35.8 us; the launch traced here: 35.7 us
  Pallas kernels  34.9 us (97%)
  local copies, waits for them, and re-layouts  0.8 us (2%)
    pallas_call x1, Pallas kernels, fast_device(): pl.pallas_call(functools.partial(fast_kernel, n_seq), out_shape=jax.Shape...  34.9 us
    unnamed x1, local copies, waits for them, and re-layouts  0.8 us

profile of v2, /device:TPU:25, one launch (start us, length us, event | category | flops | bytes accessed | tf_op | source)
XLA Modules:
  0.0 35.7 jit_solution(14013138745958199844)
XLA Ops:
  0.0 34.9 %shard_map.82 = bf16[512,512]{1,0:T(8,128)(2,1)S(1)} custom-call(f32[1,4]{1,0:T(1,128)} %bitcast.9, f32[1,4]{1,0:T(1,128)} %bitcast.10, bf16[128,2048]{1,0:T(8,128)(2,1)} %hidden.1, bf16[3,2048,512]{2,1,0:T(8,128)(2,1)} %bitcast.6, bf16[2048,512]{1,0:T(8,128)(2,1)} %w_gate.1, bf16[2,4,2048]{2,1,0:T(4,128)(2,1)} %bitcast.7, bf16[3,4,512]{2,1,0:T(4,128)(2,1)} %bitcast.8, ...), custom_call_target="tpu_custom_call" | custom-call | tf_op jit(solution)/shard_map/pallas_call | solution.py:976
  34.9 0.8 %copy.10 = bf16[512,512]{1,0:T(8,128)(2,1)} copy(bf16[512,512]{1,0:T(8,128)(2,1)S(1)} %shard_map.82) | data formatting | bytes 1048576

commit v3 on v2

--- a/solution.py
+++ b/solution.py
@@ -622,19 +622,31 @@
             low_k = low(k)
             keys[c, h] = low_k
             mixing = low(jnp.where(across < down, decays[c, h] * dot(low_k, low_k, NT), 0.0))
-            chains.append((c, h, mixing, low(k * runs[c, h]), low(k * betas[c, h]), branch(1, h, r0)))
+            chains.append((c, h, mixing, low(k * runs[c, h]), low(k * betas[c, h])))
         return chains
 
-    def solve(chains):
-        inverse = [eye - mixing * masks[0] for _, _, mixing, _, _, _ in chains]
+    def project_values(block, at, part):
+        size = heads * dim // 2
+        full = jnp.dot(block, weights[1, :, pl.ds(part * size, size)], preferred_element_type=jnp.float32)
+        full = full.astype(jnp.bfloat16).astype(jnp.float32)
+        for i in range(heads // 2):
+            got = full[:, i * dim : (i + 1) * dim]
+            proj_v[part * (heads // 2) + i, pl.ds(pl.multiple_of(at + RIM, RIM), rows), :] = got
+
+    def solve(chains, values=None):
+        inverse = [eye - mixing * masks[0] for _, _, mixing, _, _ in chains]
         for level in (1, 2):
             step = [low(dot(d, item[2] * masks[level])) for d, item in zip(inverse, chains)]
+            if values and level == 1:
+                project_values(*values, 0)
             both = [dot(x, jnp.concatenate([low(d), x], axis=1)) for x, d in zip(step, inverse)]
+            if values and level == 1:
+                project_values(*values, 1)
             first = [d.astype(jnp.float32) - p[:, :CHUNK] for p, d in zip(both, inverse)]
             inverse = [q + dot(p[:, CHUNK:], q) for p, q in zip(both, first)]
         both = [
-            dot(d, jnp.concatenate([mixing * masks[3], v, k_run], axis=1))
-            for d, (_, _, mixing, k_run, _, v) in zip(inverse, chains)
+            dot(d, jnp.concatenate([mixing * masks[3], branch(1, h, pl.multiple_of(c * CHUNK, CHUNK)), k_run], axis=1))
+            for d, (c, h, mixing, k_run, _) in zip(inverse, chains)
         ]
         again = [dot(p[:, :CHUNK], p) for p in both]
         first = [p[:, CHUNK:] - a[:, CHUNK:] for p, a in zip(both, again)]
@@ -715,10 +727,18 @@
     for piece in range(3):
         relay_copy(piece).wait_recv()
     block, places = take(((peers[3], 0, rows),))
+    project(block, range(1), places)
     gate_rows(peers[3])
-    project(block, range(2), places)
-    solve(prepare(peers[3]))
+    solve(prepare(peers[3]), (block, places[0][2]))
+    for h in range(heads):
+        fade_out[h] = fades[0, h] * fades[1, h] * (fades[2, h] * fades[3, h])
     pair_up(1 - me // 2)
+    for h in range(heads):
+        whole, fade = join((pairs[1, h], pair_fades[1, h]), (pairs[0, h], pair_fades[0, h]))
+        joined_b[h] = whole[:, :dim]
+        joined[h] = whole[:, dim:]
+        joined_f[h] = fade
+        map_out[h] = low(whole)
 
     def map_copy(h):
         return pltpu.make_async_remote_copy(
@@ -764,12 +784,9 @@
 
     @pl.when(even)
     def _():
-        for h in range(heads):
-            whole, fade = join((pairs[1, h], pair_fades[1, h]), (pairs[0, h], pair_fades[0, h]))
-            map_out[h] = low(whole)
-            fade_out[h] = fade
+        fade_copy().start()
+        for h in range(heads):
             map_copy(h).start()
-        fade_copy().start()
 
     @pl.when(seq == 0)
     def _():
@@ -785,31 +802,27 @@
 
         return send
 
-    def whole_map(h):
-        return join((pairs[1, h], pair_fades[1, h]), (pairs[0, h], pair_fades[0, h]))
-
     def sent_map(h):
         return map_in[h].astype(jnp.float32), fade_in[h]
 
     def begin(skip):
-        mine = [whole_map(h) for h in range(heads)]
+        for h in range(heads):
+            map_copy(h).wait_recv()
+            state = map_in[h, :, :dim]
+            base = joined_f[h] * state.astype(jnp.float32) + joined_b[h]
+            st_out[h] = low(base + dot(joined[h], state))
+            send_on(skip)(h)
         fade_copy().wait_recv()
-        for h in range(heads):
-            map_copy(h).wait_recv()
-            (whole, fade), state = mine[h], map_in[h, :, :dim]
-            base = fade * state.astype(jnp.float32) + whole[:, :dim]
-            st_out[h] = low(base + dot(whole[:, dim:], state))
-            send_on(skip)(h)
         for h in range(heads):
             held[h] = map_in[h, :, :dim]
             if skip:
                 state_copy(h).start()
 
-    def compose():
-        mine = [whole_map(h) for h in range(heads)]
+    def compose(ends):
         fade_copy().wait_recv()
         for h in range(heads):
             map_copy(h).wait_recv()
+        mine = [(jnp.concatenate([joined_b[h], joined[h]], axis=1), joined_f[h]) for h in range(heads)]
         both = [join(mine[h], sent_map(h)) for h in range(heads)]
         for h, (whole, fade) in enumerate(both):
             joined_b[h] = whole[:, :dim]
@@ -817,19 +830,14 @@
             joined_f[h] = fade
             map_out[h] = low(whole)
 
-        @pl.when(seq == last_seq - 2)
-        def _():
+        if ends:
+            far_fade_copy().start()
             for h in range(heads):
                 far_copy(h).start()
-            far_fade_copy().start()
 
     @pl.when(seq == 1)
     def _():
         begin(last_seq == 5)
-
-    @pl.when(jnp.logical_and(jnp.logical_and(odd, seq > 1), seq < last_seq))
-    def _():
-        compose()
 
     def carry(h, state, whole, fade):
         wide = state.astype(jnp.float32)
@@ -851,26 +859,29 @@
 
     def end_chain():
         fade_copy().wait_recv()
+        for h in range(heads):
+            map_copy(h).wait_recv()
         far_fade_copy().wait_recv()
         for h in range(heads):
-            map_copy(h).wait_recv()
             far_copy(h).wait_recv()
-        for h in range(heads):
-            whole, fade = join(sent_map(h), (far_in[h].astype(jnp.float32), far_fade[h]))
-            joined_b[h] = whole[:, :dim]
-            joined[h] = whole[:, dim:]
-            joined_f[h] = fade
-        for h in range(heads):
             state_copy(h).wait_recv()
-            state = st_in[h]
-            st_out[h] = carry(h, state, far_in[h], far_fade[h])
+            st_out[h] = carry(h, st_in[h], far_in[h], far_fade[h])
             share_copy(h, st_out).start()
-            wide = joined_f[h] * state.astype(jnp.float32) + joined_b[h]
-            held[h] = low(wide + dot(joined[h], state))
+        for h in range(heads):
+            held[h] = carry(h, st_out[h], map_in[h], fade_in[h])
+
+    @pl.when(seq == last_seq - 2)
+    def _():
+        compose(True)
 
     project(late, range(2, 4), late_places)
+
+    @pl.when(jnp.logical_and(jnp.logical_and(odd, seq > 1), seq < last_seq - 2))
+    def _():
+        compose(False)
+
+
     queries(peers[1])
-    queries(peers[2])
 
     @pl.when(jnp.logical_and(jnp.logical_and(odd, seq > 1), seq < last_seq - 4))
     def _():
@@ -882,9 +893,13 @@
         def _():
             pass_on(True, True)
 
+    queries(peers[2])
+
+
     project(block, range(2, 4), places)
     queries(peers[3])
     for h in range(heads):
+        gates[h] = half_silu(0.5 * gates[h]) * gain_ref[...]
         third, fade = join((maps[2, h], fades[2, h]), (pairs[0, h], pair_fades[0, h]))
         for c in range(count):
             at = pl.ds(c * CHUNK, CHUNK)
@@ -917,7 +932,7 @@
         cols = slice(h * dim, (h + 1) * dim)
         read = outs[h] + dot(deltas[h], held[h])
         scale = lax.rsqrt(jnp.mean(read * read, axis=-1, keepdims=True) + 1e-06)
-        out_ref[:, cols] = low(read * scale * gain_ref[...] * half_silu(0.5 * gates[h]))
+        out_ref[:, cols] = low(read * scale * gates[h])
 
     for step in range(1, 4):
         for piece in range(4):

time: 35.8 us -> 34.6 us (0.966)
  Pallas kernels: 34.9 us -> 33.6 us
    pallas_call x1, Pallas kernels: 34.9 us -> 33.6 us  [fast_device(): pl.pallas_call(functools.partial(fast_kernel, n_seq), out_shape=jax.Shape...]
where the time goes in v3:
time: 34.6 us; the launch traced here: 34.4 us
  Pallas kernels  33.6 us (97%)
  local copies, waits for them, and re-layouts  0.8 us (2%)
    pallas_call x1, Pallas kernels, fast_device(): pl.pallas_call(functools.partial(fast_kernel, n_seq), out_shape=jax.Shape...  33.6 us
    unnamed x1, local copies, waits for them, and re-layouts  0.8 us

profile of v3, /device:TPU:25, one launch (start us, length us, event | category | flops | bytes accessed | tf_op | source)
XLA Modules:
  0.0 34.4 jit_solution(1091099873279338366)
XLA Ops:
  0.0 33.6 %shard_map.82 = bf16[512,512]{1,0:T(8,128)(2,1)S(1)} custom-call(f32[1,4]{1,0:T(1,128)} %bitcast.9, f32[1,4]{1,0:T(1,128)} %bitcast.10, bf16[128,2048]{1,0:T(8,128)(2,1)} %hidden.1, bf16[3,2048,512]{2,1,0:T(8,128)(2,1)} %bitcast.6, bf16[2048,512]{1,0:T(8,128)(2,1)} %w_gate.1, bf16[2,4,2048]{2,1,0:T(4,128)(2,1)} %bitcast.7, bf16[3,4,512]{2,1,0:T(4,128)(2,1)} %bitcast.8, ...), custom_call_target="tpu_custom_call" | custom-call | tf_op jit(solution)/shard_map/pallas_call | solution.py:991
  33.6 0.8 %copy.10 = bf16[512,512]{1,0:T(8,128)(2,1)} copy(bf16[512,512]{1,0:T(8,128)(2,1)S(1)} %shard_map.82) | data formatting | bytes 1048576
